TPU v7x, 256 devices: a 4x2x16 block of a 4x16x16 slice. The times are simulated.
256 devices in a mesh: groups: 2 (over y), dp: 16 (over z), section: 4 (over x), tensor: 2 (over core).
Axes of the slice: x: 4, y: 2, z: 16, core: 2. Of those that a mesh axis runs over, the one named last changes fastest.
The devices are a block of a 4x16x16 slice.
Arguments:
- hidden: bfloat16 [512, 8, 5120], P(('groups', 'dp')), parts along dimension 0, may hold values from -6 to 6
- unembed: bfloat16 [512, 8, 5120], P(('groups', 'dp')), parts along dimension 0, may hold values from -0.02734375 to 0.02734375
- value_proj: bfloat16 [4, 5120, 512], P('section', 'dp', 'tensor'), may hold values from -0.078125 to 0.078125
- output_proj: bfloat16 [4, 512, 5120], P('section', 'tensor', 'dp'), may hold values from -0.125 to 0.125
- norm_gains: float32 [4, 5120], P('section'), may hold values from 0.1 to 1.9
- survive: int32 [32], P(('groups', 'dp')), parts along dimension 0, may hold values from 0 to 1, as said below
- lengths: int32 [512], P(('groups', 'dp')), parts along dimension 0, may hold values from 1 to 8
- assign: int32 [512], P(('groups', 'dp')), parts along dimension 0, may hold values from 0 to 16, as said below
- advantage: float32 [512], P(('groups', 'dp')), parts along dimension 0, may hold values from -4 to 4
- reference_logit: float32 [512, 8], P(('groups', 'dp')), parts along dimension 0, may hold values from -4 to 4
- recorded_gap: float32 [512, 8], P(('groups', 'dp')), parts along dimension 0, may hold values from -2 to 2
Outputs:
- grad_value: float32 [8, 5120, 512], P(('groups', 'section'), 'dp', 'tensor'), parts along dimension 0
- grad_output: float32 [8, 512, 5120], P(('groups', 'section'), 'tensor', 'dp'), parts along dimension 0
There are 2 independent parts, one for each index of `groups`. A program takes and returns all parts, laid end to end along the dimension named above; an argument that names none is the same for every part. Nothing has to cross between parts.
Inputs may be any that keep to these rules, and one draw needn't show every extreme that they name: `survive`: 1 where the group of 16 responses is kept, 0 where it is dropped; in every draw all groups of some dp index are kept. `assign`: the 16 slots of a dp index list the local positions (0 to 15) of the responses of its kept groups, each exactly once, then hold 16 in every other slot.
All inputs are finite; a program needn't handle non-finite values.
Results may differ from a plain program's by a relative error of at most 0.029.
Values may be sent and summed in bfloat16 or wider, within the bound.
A program may use at most 64 MiB of HBM per device.

v0:
```python
import math
import jax
import jax.numpy as jnp
from jax import lax
from jax.sharding import PartitionSpec as P

GROUP = 16
MB_RESP = 8
eps_norm = 1e-06
loss_scale = 4096.0
clip_high = math.log(1.28)
clip_low = math.log(0.8)


def turned_gather(arrays, axis, dims):
    turned = [jnp.moveaxis(a, dim, 0) for a, dim in zip(arrays, dims)]
    widths = [t[0].size for t in turned]
    both = jnp.concatenate([t.reshape(-1, w) for t, w in zip(turned, widths)], axis=1)
    result = lax.all_gather(both, axis, axis=0, tiled=True)
    tiles = jnp.split(result, [sum(widths[:k]) for k in range(1, len(widths))], axis=1)
    return tuple(
        (
            jnp.moveaxis(b.reshape(-1, *t.shape[1:]), 0, dim)
            for b, t, dim in zip(tiles, turned, dims)
        )
    )


def copy_for_each(array, axis):
    devices = lax.axis_size(axis)
    return lax.all_to_all(
        jnp.broadcast_to(array[None], (devices, *array.shape)), axis, 0, 0, tiled=True
    )


def taken_together(array, axis):
    return copy_for_each(array, axis).astype(jnp.float32).sum(axis=0)


def from_behind(block, axis, distance):
    devices = range(lax.axis_size(axis))
    route = [(i - distance, i) for i in devices if i - distance in devices]
    return lax.ppermute(block, axis, route)


def of_everyone(array, axis):
    everything = copy_for_each(array, axis)
    return jnp.sum(everything, axis=0)


def norm_forward(row_block, norm_gain):
    values = row_block.astype(jnp.float32)
    inverse = lax.rsqrt(jnp.mean(values * values, axis=-1, keepdims=True) + eps_norm)
    return (values, inverse, (values * inverse * norm_gain).astype(jnp.bfloat16))


def norm_backward(values, inverse, norm_gain, upstream):
    scaled = upstream * norm_gain
    inner_sum = jnp.sum(scaled * values, axis=-1, keepdims=True) / values.shape[-1]
    return inverse * scaled - values * (inverse * inverse * inverse) * inner_sum


def contract_last(left_rows, right_rows):
    return lax.dot_general(
        left_rows, right_rows, (((1,), (1,)), ((), ())), preferred_element_type=jnp.float32
    )


def contract_first(left_rows, right_rows):
    return lax.dot_general(
        left_rows, right_rows, (((0,), (0,)), ((), ())), preferred_element_type=jnp.float32
    )


def take_slot(slot_store, slot_index):
    return lax.dynamic_index_in_dim(slot_store, slot_index, 0, keepdims=False)


def put_slot(slot_store, new_value, slot_index, active):
    previous = take_slot(slot_store, slot_index)
    return lax.dynamic_update_index_in_dim(
        slot_store, jnp.where(active, new_value, previous), slot_index, 0
    )


def local(
    hidden,
    unembed,
    value_proj,
    output_proj,
    norm_gains,
    survive,
    lengths,
    assign,
    advantage,
    reference_logit,
    recorded_gap,
):
    resp_count = hidden.shape[0]
    positions = hidden.shape[1]
    model_width = hidden.shape[2]
    half_value = value_proj.shape[2]
    micro_count = resp_count // MB_RESP
    row_count = MB_RESP * positions
    section_count = lax.axis_size("section")
    section_index = lax.axis_index("section")
    is_last = section_index == section_count - 1
    norm_gain = norm_gains[0]
    alive_mask = jnp.repeat(survive, GROUP)
    local_count = jnp.sum((alive_mask * lengths).astype(jnp.float32))
    gathered_value, gathered_output = turned_gather((value_proj, output_proj), "dp", (1, 2))
    w_first = gathered_value[0]
    w_second = gathered_output[0]

    def pick(array):
        return jnp.take(array, assign, axis=0, mode="fill", fill_value=0)

    slot_hidden = pick(hidden).reshape(micro_count, row_count, model_width)
    slot_unembed = pick(unembed).reshape(micro_count, row_count, model_width)
    position_index = lax.broadcasted_iota(jnp.int32, (resp_count, positions), 1)
    live_mask = (position_index < pick(lengths)[:, None]).astype(jnp.float32)
    advantages = jnp.broadcast_to(pick(advantage)[:, None], (resp_count, positions))
    gap_rows = pick(recorded_gap)
    clipped = (advantages > 0) & (gap_rows > clip_high) | (advantages < 0) & (gap_rows < clip_low)
    kept_mask = 1.0 - clipped.astype(jnp.float32)
    weight_rows = (-loss_scale * advantages * kept_mask * live_mask).reshape(micro_count, row_count)
    logit_base = pick(reference_logit).reshape(micro_count, row_count)
    step_count = micro_count + section_count - 1
    store_in = jnp.zeros((micro_count, row_count, model_width), jnp.bfloat16)
    store_normed = jnp.zeros((micro_count, row_count, model_width), jnp.bfloat16)
    store_projected = jnp.zeros((micro_count, row_count, half_value), jnp.bfloat16)
    store_out = jnp.zeros((micro_count, row_count, model_width), jnp.bfloat16)
    arriving = jnp.zeros((row_count, model_width), jnp.bfloat16)
    for step_index in range(step_count):
        micro_index = step_index - section_index
        active = (micro_index >= 0) & (micro_index < micro_count)
        clamped = jnp.clip(micro_index, 0, micro_count - 1)
        entering = jnp.where(section_index == 0, take_slot(slot_hidden, clamped), arriving)
        values, inverse, normed = norm_forward(entering, norm_gain)
        projected = jnp.dot(normed, w_first, preferred_element_type=jnp.float32).astype(
            jnp.bfloat16
        )
        partial_out = jnp.dot(projected, w_second, preferred_element_type=jnp.float32)
        mixed_sum = taken_together(partial_out.astype(jnp.bfloat16), "tensor").astype(jnp.float32)
        leaving = (values + mixed_sum).astype(jnp.bfloat16)
        store_in = put_slot(store_in, entering, clamped, active)
        store_normed = put_slot(store_normed, normed, clamped, active)
        store_projected = put_slot(store_projected, projected, clamped, active)
        store_out = put_slot(store_out, leaving, clamped, active)
        arriving = from_behind(leaving, "section", 1)
    store_upstream = jnp.zeros((micro_count, row_count, model_width), jnp.bfloat16)
    store_grad_value = jnp.zeros((micro_count, row_count, half_value), jnp.bfloat16)
    arriving = jnp.zeros((row_count, model_width), jnp.bfloat16)
    for step_index in range(step_count):
        micro_index = step_index - (section_count - 1 - section_index)
        active = (micro_index >= 0) & (micro_index < micro_count)
        clamped = jnp.clip(micro_index, 0, micro_count - 1)
        top_rows = take_slot(store_out, clamped).astype(jnp.float32)
        unembed_rows = take_slot(slot_unembed, clamped).astype(jnp.float32)
        logit = jnp.sum(top_rows * unembed_rows, axis=-1)
        seed_rows = take_slot(weight_rows, clamped) * jnp.exp(
            logit - take_slot(logit_base, clamped)
        )
        start_grad = (seed_rows[:, None] * unembed_rows).astype(jnp.bfloat16)
        upstream = jnp.where(is_last, start_grad, arriving)
        entering = take_slot(store_in, clamped)
        normed = take_slot(store_normed, clamped)
        projected = take_slot(store_projected, clamped)
        grad_projected = contract_last(upstream, w_second).astype(jnp.bfloat16)
        partial_norm = contract_last(grad_projected, w_first)
        grad_normed = taken_together(partial_norm.astype(jnp.bfloat16), "tensor").astype(
            jnp.float32
        )
        values, inverse, unused_normed = norm_forward(entering, norm_gain)
        grad_entering = (
            upstream.astype(jnp.float32) + norm_backward(values, inverse, norm_gain, grad_normed)
        ).astype(jnp.bfloat16)
        store_upstream = put_slot(store_upstream, upstream, clamped, active)
        store_grad_value = put_slot(store_grad_value, grad_projected, clamped, active)
        arriving = from_behind(grad_entering, "section", -1)
    flat_normed = store_normed.reshape(micro_count * row_count, model_width)
    flat_upstream = store_upstream.reshape(micro_count * row_count, model_width)
    flat_grad_value = store_grad_value.reshape(micro_count * row_count, half_value)
    flat_projected = store_projected.reshape(micro_count * row_count, half_value)
    reduced = lax.psum_scatter(
        jnp.concatenate(
            [
                contract_first(flat_normed, flat_grad_value),
                contract_first(flat_upstream, flat_projected),
            ],
            axis=1,
        ).astype(jnp.bfloat16),
        "dp",
        scatter_dimension=0,
        tiled=True,
    ).astype(jnp.float32)
    token_total = of_everyone(local_count, "dp")
    scaled_grads = reduced / token_total
    grad_value = scaled_grads[:, :half_value][None]
    grad_output = scaled_grads[:, half_value:].T[None]
    return (grad_value, grad_output)


def solution(mesh):
    placed = (
        P(("groups", "dp"), None, None),
        P(("groups", "dp"), None, None),
        P("section", "dp", "tensor"),
        P("section", "tensor", "dp"),
        P("section", None),
        P(("groups", "dp")),
        P(("groups", "dp")),
        P(("groups", "dp")),
        P(("groups", "dp")),
        P(("groups", "dp"), None),
        P(("groups", "dp"), None),
    )
    return jax.shard_map(
        local,
        mesh=mesh,
        in_specs=placed,
        out_specs=(
            P(("groups", "section"), "dp", "tensor"),
            P(("groups", "section"), "tensor", "dp"),
        ),
        check_vma=False,
    )
```

profile of v0, /device:TPU:34, one launch (start us, length us, event | category | flops | bytes accessed | tf_op | source)
XLA Modules:
  0.0 454.4 jit_solution(10710032838537592977)
XLA Ops:
  11.3 3.1 gather_fusion.4
  16.6 2.7 broadcast_select_fusion.1
  20.5 82.5 %all-gather.2.cloned.1.call-done = bf16[5120,512]{1,0:T(8,128)(2,1)} async-done(((bf16[320,512]{1,0:T(8,128)(2,1)}), bf16[5120,512]{1,0:T(8,128)(2,1)}) %all-gather.2.cloned.1.call-update) | async-done | bytes 5242896 | tf_op jit(solution)/shard_map/all_gather | solution.py:19
  103.0 2.6 bitcast_dynamic-update-slice_fusion.19
  105.6 2.6 convolution_convert_fusion.8
  108.4 4.9 %all_to_all.51 = bf16[2,64,5120]{2,1,0:T(8,128)(2,1)S(1)} all-to-all(bf16[2,64,5120]{2,1,0:T(8,128)(2,1)S(1)} %broadcast_in_dim.204), channel_id=1, replica_groups=mesh['groups'=2,'dp'=16,'section'=4,'tensor'=2] {'tensor'}, dimensions={0} | all-to-all | bytes 2621440 | tf_op jit(solution)/shard_map/all_to_all | solution.py:31
  113.7 3.8 collective-permute-start
  117.7 15.0 %collective-permute-done = bf16[64,5120]{1,0:T(8,128)(2,1)S(1)} collective-permute-done((bf16[64,5120]{1,0:T(8,128)(2,1)S(1)}, bf16[64,5120]{1,0:T(8,128)(2,1)S(1)}, u32[]{:S(2)}, u32[]{:S(2)}) %collective-permute-start) | collective-permute-done | bytes 655392 | tf_op jit(solution)/shard_map/ppermute | solution.py:43
  137.1 4.5 %all-to-all-start.1 = ((bf16[2,64,5120]{2,1,0:T(8,128)(2,1)}), bf16[2,64,5120]{2,1,0:T(8,128)(2,1)}, u32[]{:S(2)}, u32[]{:S(2)}) async-start(bf16[2,64,5120]{2,1,0:T(8,128)(2,1)} %broadcast_in_dim.206), calls=%async_computation.1 | async-start | bytes 2621440 | tf_op jit(solution)/shard_map/all_to_all | solution.py:31
  146.2 3.8 collective-permute-start.1
  150.2 15.0 %collective-permute-done.1 = bf16[64,5120]{1,0:T(8,128)(2,1)S(1)} collective-permute-done((bf16[64,5120]{1,0:T(8,128)(2,1)S(1)}, bf16[64,5120]{1,0:T(8,128)(2,1)S(1)}, u32[]{:S(2)}, u32[]{:S(2)}) %collective-permute-start.1) | collective-permute-done | bytes 655392 | tf_op jit(solution)/shard_map/ppermute | solution.py:43
  167.4 4.8 %all_to_all.52 = bf16[2,64,5120]{2,1,0:T(8,128)(2,1)S(1)} all-to-all(bf16[2,64,5120]{2,1,0:T(8,128)(2,1)S(1)} %broadcast_in_dim.208), channel_id=1, replica_groups=mesh['groups'=2,'dp'=16,'section'=4,'tensor'=2] {'tensor'}, dimensions={0} | all-to-all | bytes 2621440 | tf_op jit(solution)/shard_map/all_to_all | solution.py:31
  172.8 3.6 collective-permute-start.2
  176.5 15.0 %collective-permute-done.2 = bf16[64,5120]{1,0:T(8,128)(2,1)S(1)} collective-permute-done((bf16[64,5120]{1,0:T(8,128)(2,1)S(1)}, bf16[64,5120]{1,0:T(8,128)(2,1)S(1)}, u32[]{:S(2)}, u32[]{:S(2)}) %collective-permute-start.2) | collective-permute-done | bytes 655392 | tf_op jit(solution)/shard_map/ppermute | solution.py:43
  193.8 4.8 %all_to_all.53 = bf16[2,64,5120]{2,1,0:T(8,128)(2,1)S(1)} all-to-all(bf16[2,64,5120]{2,1,0:T(8,128)(2,1)S(1)} %broadcast_in_dim.210), channel_id=1, replica_groups=mesh['groups'=2,'dp'=16,'section'=4,'tensor'=2] {'tensor'}, dimensions={0} | all-to-all | bytes 2621440 | tf_op jit(solution)/shard_map/all_to_all | solution.py:31
  199.1 3.8 collective-permute-start.3
  203.9 13.9 %collective-permute-done.3 = bf16[64,5120]{1,0:T(8,128)(2,1)S(1)} collective-permute-done((bf16[64,5120]{1,0:T(8,128)(2,1)S(1)}, bf16[64,5120]{1,0:T(8,128)(2,1)S(1)}, u32[]{:S(2)}, u32[]{:S(2)}) %collective-permute-start.3) | collective-permute-done | bytes 655392 | tf_op jit(solution)/shard_map/ppermute | solution.py:43
  223.9 4.6 %all-to-all-start.4 = ((bf16[2,64,5120]{2,1,0:T(8,128)(2,1)}), bf16[2,64,5120]{2,1,0:T(8,128)(2,1)}, u32[]{:S(2)}, u32[]{:S(2)}) async-start(bf16[2,64,5120]{2,1,0:T(8,128)(2,1)} %broadcast_in_dim.219), calls=%async_computation.4 | async-start | bytes 2621440 | tf_op jit(solution)/shard_map/all_to_all | solution.py:31
  239.4 2.6 bitcast_dynamic-update-slice_fusion.11
  244.7 4.8 %all_to_all.54 = bf16[2,64,5120]{2,1,0:T(8,128)(2,1)S(1)} all-to-all(bf16[2,64,5120]{2,1,0:T(8,128)(2,1)S(1)} %broadcast_in_dim.226), channel_id=1, replica_groups=mesh['groups'=2,'dp'=16,'section'=4,'tensor'=2] {'tensor'}, dimensions={0} | all-to-all | bytes 2621440 | tf_op jit(solution)/shard_map/all_to_all | solution.py:31
  254.6 16.2 %collective-permute-done.4 = bf16[64,5120]{1,0:T(8,128)(2,1)S(1)} collective-permute-done((bf16[64,5120]{1,0:T(8,128)(2,1)S(1)}, bf16[64,5120]{1,0:T(8,128)(2,1)S(1)}, u32[]{:S(2)}, u32[]{:S(2)}) %collective-permute-start.4) | collective-permute-done | bytes 655392 | tf_op jit(solution)/shard_map/ppermute | solution.py:43
  272.9 4.8 %all_to_all.55 = bf16[2,64,5120]{2,1,0:T(8,128)(2,1)S(1)} all-to-all(bf16[2,64,5120]{2,1,0:T(8,128)(2,1)S(1)} %broadcast_in_dim.228), channel_id=1, replica_groups=mesh['groups'=2,'dp'=16,'section'=4,'tensor'=2] {'tensor'}, dimensions={0} | all-to-all | bytes 2621440 | tf_op jit(solution)/shard_map/all_to_all | solution.py:31
  278.7 2.5 collective-permute-start.5
  281.2 16.2 %collective-permute-done.5 = bf16[64,5120]{1,0:T(8,128)(2,1)S(1)} collective-permute-done((bf16[64,5120]{1,0:T(8,128)(2,1)S(1)}, bf16[64,5120]{1,0:T(8,128)(2,1)S(1)}, u32[]{:S(2)}, u32[]{:S(2)}) %collective-permute-start.5) | collective-permute-done | bytes 655392 | tf_op jit(solution)/shard_map/ppermute | solution.py:43
  299.4 4.8 %all_to_all.56 = bf16[2,64,5120]{2,1,0:T(8,128)(2,1)S(1)} all-to-all(bf16[2,64,5120]{2,1,0:T(8,128)(2,1)S(1)} %broadcast_in_dim.230), channel_id=1, replica_groups=mesh['groups'=2,'dp'=16,'section'=4,'tensor'=2] {'tensor'}, dimensions={0} | all-to-all | bytes 2621440 | tf_op jit(solution)/shard_map/all_to_all | solution.py:31
  307.5 16.4 %collective-permute-done.6 = bf16[64,5120]{1,0:T(8,128)(2,1)S(1)} collective-permute-done((bf16[64,5120]{1,0:T(8,128)(2,1)S(1)}, bf16[64,5120]{1,0:T(8,128)(2,1)S(1)}, u32[]{:S(2)}, u32[]{:S(2)}) %collective-permute-start.6) | collective-permute-done | bytes 655392 | tf_op jit(solution)/shard_map/ppermute | solution.py:43
  325.9 4.8 %all_to_all.57 = bf16[2,64,5120]{2,1,0:T(8,128)(2,1)S(1)} all-to-all(bf16[2,64,5120]{2,1,0:T(8,128)(2,1)S(1)} %broadcast_in_dim.232), channel_id=1, replica_groups=mesh['groups'=2,'dp'=16,'section'=4,'tensor'=2] {'tensor'}, dimensions={0} | all-to-all | bytes 2621440 | tf_op jit(solution)/shard_map/all_to_all | solution.py:31
  334.0 16.4 %collective-permute-done.7 = bf16[64,5120]{1,0:T(8,128)(2,1)S(1)} collective-permute-done((bf16[64,5120]{1,0:T(8,128)(2,1)S(1)}, bf16[64,5120]{1,0:T(8,128)(2,1)S(1)}, u32[]{:S(2)}, u32[]{:S(2)}) %collective-permute-start.7) | collective-permute-done | bytes 655392 | tf_op jit(solution)/shard_map/ppermute | solution.py:43
  354.6 2.7 pad_maximum_fusion
  357.3 7.9 %copy.34 = bf16[5120,512]{1,0:T(8,128)(2,1)} copy(bf16[5120,512]{0,1:T(8,128)(2,1)} %pad_maximum_fusion) | data formatting | bytes 10485760
  367.2 19.5 %all_to_all.58 = f32[16,1,1]{2,1,0:T(1,128)S(1)} all-to-all(f32[16,1,1]{2,1,0:T(1,128)S(1)} %broadcast_in_dim.243), channel_id=1, replica_groups=mesh['groups'=2,'dp'=16,'section'=4,'tensor'=2] {'dp'}, dimensions={0} | all-to-all | bytes 128 | tf_op jit(solution)/shard_map/all_to_all | solution.py:31
  387.3 56.4 %reduce-scatter.4.cloned.1.call-done = bf16[320,512]{1,0:T(8,128)(2,1)} async-done(((bf16[5120,512]{1,0:T(8,128)(2,1)}), bf16[320,512]{1,0:T(8,128)(2,1)}) %reduce-scatter.4.cloned.1.call-update) | async-done | bytes 327696
  (210 shorter events, 71.7 us)
Async XLA Ops:
  7.2 3.4 copy-start
  7.2 2.7 copy-start.2
  7.2 95.8 %all-gather.2.cloned.1.call-start = ((), (), s32[]{:S(2)}) async-start(), calls=%async_computation.11 | async-start | bytes 5570560 | tf_op jit(solution)/shard_map/all_gather | solution.py:19
  11.2 3.1 copy-start.3
  11.2 3.8 copy-start.22
  11.2 4.4 copy-start.23
  11.2 5.0 %copy-start.24 = (s32[16]{0:T(128)S(1)}, s32[16]{0:T(128)}, u32[]{:S(2)}) copy-start(s32[16]{0:T(128)} %param.22) | copy-start | bytes 196
  19.5 83.5 %copy-start.20 = (f32[1,5120]{1,0:T(1,128)S(1)}, f32[1,5120]{1,0:T(1,128)}, u32[]{:S(2)}) copy-start(f32[1,5120]{1,0:T(1,128)} %param.19) | copy-start | bytes 61444
  108.4 5.2 %copy-start.14 = (bf16[16,8,5120]{2,1,0:T(8,128)(2,1)S(1)}, bf16[16,8,5120]{2,1,0:T(8,128)(2,1)}, u32[]{:S(2)}) copy-start(bf16[16,8,5120]{2,1,0:T(8,128)(2,1)} %copy-done.13) | copy-start | bytes 3932164
  113.3 20.3 %slice-start = ((s8[5242880]{0:T(1024)(128)(4,1)}), s8[4194304]{0:T(1024)(128)(4,1)S(1)}, s32[]{:S(2)}) async-start(s8[5242880]{0:T(1024)(128)(4,1)} %bitcast.385), calls=%async_computation.13 | async-start | bytes 8388608
  113.7 19.0 %collective-permute-start = (bf16[64,5120]{1,0:T(8,128)(2,1)S(1)}, bf16[64,5120]{1,0:T(8,128)(2,1)S(1)}, u32[]{:S(2)}, u32[]{:S(2)}) collective-permute-start(bf16[64,5120]{1,0:T(8,128)(2,1)S(1)} %fusion.21), channel_id=1, source_target_pairs={{0,2},{2,4},{4,6},{1,3},{3,5},{5,7},{8,10},{10,12},{12,14},{9,11},... | collective-permute-start | bytes 1966088 | tf_op jit(solution)/shard_map/ppermute | solution.py:43
  117.7 16.0 %slice-start.1 = ((s8[5242880]{0:T(1024)(128)(4,1)}), s8[1048576]{0:T(1024)(128)(4,1)S(1)}, s32[]{:S(2)}) async-start(s8[5242880]{0:T(1024)(128)(4,1)} %bitcast.385), calls=%async_computation.14 | async-start | bytes 2097152
  137.1 7.0 %all-to-all-start.1 = ((bf16[2,64,5120]{2,1,0:T(8,128)(2,1)}), bf16[2,64,5120]{2,1,0:T(8,128)(2,1)}, u32[]{:S(2)}, u32[]{:S(2)}) async-start(bf16[2,64,5120]{2,1,0:T(8,128)(2,1)} %broadcast_in_dim.206), calls=%async_computation.1 | async-start | bytes 2621440 | tf_op jit(solution)/shard_map/all_to_all | solution.py:31
  141.6 24.1 %slice-start.2 = ((s8[5242880]{0:T(1024)(128)(4,1)}), s8[1048576]{0:T(1024)(128)(4,1)S(1)}, s32[]{:S(2)}) async-start(s8[5242880]{0:T(1024)(128)(4,1)} %bitcast.387), calls=%async_computation.15 | async-start | bytes 2097152
  144.0 6.0 %copy-start.5 = (bf16[2,64,5120]{2,1,0:T(8,128)(2,1)S(1)}, bf16[2,64,5120]{2,1,0:T(8,128)(2,1)}, u32[]{:S(2)}) copy-start(bf16[2,64,5120]{2,1,0:T(8,128)(2,1)} %copy-done.4) | copy-start | bytes 3932164
  145.9 19.9 %slice-start.3 = ((s8[5242880]{0:T(1024)(128)(4,1)}), s8[4194304]{0:T(1024)(128)(4,1)S(1)}, s32[]{:S(2)}) async-start(s8[5242880]{0:T(1024)(128)(4,1)} %bitcast.387), calls=%async_computation.16 | async-start | bytes 8388608
  146.2 19.0 %collective-permute-start.1 = (bf16[64,5120]{1,0:T(8,128)(2,1)S(1)}, bf16[64,5120]{1,0:T(8,128)(2,1)S(1)}, u32[]{:S(2)}, u32[]{:S(2)}) collective-permute-start(bf16[64,5120]{1,0:T(8,128)(2,1)S(1)} %get-tuple-element.43), channel_id=1, source_target_pairs={{0,2},{2,4},{4,6},{1,3},{3,5},{5,7},{8,10},{10,12},{12,14},{9,11},... | collective-permute-start | bytes 1966088 | tf_op jit(solution)/shard_map/ppermute | solution.py:43
  150.1 15.1 %copy-start.15 = (bf16[16,8,5120]{2,1,0:T(8,128)(2,1)S(1)}, bf16[16,8,5120]{2,1,0:T(8,128)(2,1)}, u32[]{:S(2)}) copy-start(bf16[16,8,5120]{2,1,0:T(8,128)(2,1)} %copy-done.13) | copy-start | bytes 3932164
  172.8 18.7 %collective-permute-start.2 = (bf16[64,5120]{1,0:T(8,128)(2,1)S(1)}, bf16[64,5120]{1,0:T(8,128)(2,1)S(1)}, u32[]{:S(2)}, u32[]{:S(2)}) collective-permute-start(bf16[64,5120]{1,0:T(8,128)(2,1)S(1)} %get-tuple-element.41), channel_id=1, source_target_pairs={{0,2},{2,4},{4,6},{1,3},{3,5},{5,7},{8,10},{10,12},{12,14},{9,11},... | collective-permute-start | bytes 1966088 | tf_op jit(solution)/shard_map/ppermute | solution.py:43
  191.8 7.0 %copy-start.16 = (bf16[64,5120]{1,0:T(8,128)(2,1)}, bf16[64,5120]{1,0:T(8,128)(2,1)S(1)}, u32[]{:S(2)}) copy-start(bf16[64,5120]{1,0:T(8,128)(2,1)S(1)} %get-tuple-element.33) | copy-start | bytes 1966084
  199.1 4.8 %copy-start.11 = (bf16[2,64,5120]{2,1,0:T(8,128)(2,1)}, bf16[2,64,5120]{2,1,0:T(8,128)(2,1)S(1)}, u32[]{:S(2)}) copy-start(bf16[2,64,5120]{2,1,0:T(8,128)(2,1)S(1)} %get-tuple-element.38) | copy-start | bytes 3932164
  199.1 18.7 %collective-permute-start.3 = (bf16[64,5120]{1,0:T(8,128)(2,1)S(1)}, bf16[64,5120]{1,0:T(8,128)(2,1)S(1)}, u32[]{:S(2)}, u32[]{:S(2)}) collective-permute-start(bf16[64,5120]{1,0:T(8,128)(2,1)S(1)} %get-tuple-element.39), channel_id=1, source_target_pairs={{0,2},{2,4},{4,6},{1,3},{3,5},{5,7},{8,10},{10,12},{12,14},{9,11},... | collective-permute-start | bytes 1966088 | tf_op jit(solution)/shard_map/ppermute | solution.py:43
  223.9 13.7 %all-to-all-start.4 = ((bf16[2,64,5120]{2,1,0:T(8,128)(2,1)}), bf16[2,64,5120]{2,1,0:T(8,128)(2,1)}, u32[]{:S(2)}, u32[]{:S(2)}) async-start(bf16[2,64,5120]{2,1,0:T(8,128)(2,1)} %broadcast_in_dim.219), calls=%async_computation.4 | async-start | bytes 2621440 | tf_op jit(solution)/shard_map/all_to_all | solution.py:31
  228.4 215.2 %reduce-scatter.4.cloned.1.call-start = ((), (), s32[]{:S(2)}) async-start(), calls=%async_computation.12 | async-start | bytes 5570560
  234.3 5.1 %copy-start.21 = (bf16[1,64,5120]{2,1,0:T(8,128)(2,1)S(1)}, bf16[1,64,5120]{2,1,0:T(8,128)(2,1)}, u32[]{:S(2)}) copy-start(bf16[1,64,5120]{2,1,0:T(8,128)(2,1)} %constant_dynamic-slice_fusion.25) | copy-start | bytes 1966084
  235.4 4.0 copy-start.12
  237.5 5.5 %slice-start.4 = ((s8[5242880]{0:T(1024)(128)(4,1)}), s8[4194304]{0:T(1024)(128)(4,1)S(1)}, s32[]{:S(2)}) async-start(s8[5242880]{0:T(1024)(128)(4,1)} %bitcast.389), calls=%async_computation.17 | async-start | bytes 8388608
  239.4 3.6 slice-start.5
  252.2 18.7 %collective-permute-start.4 = (bf16[64,5120]{1,0:T(8,128)(2,1)S(1)}, bf16[64,5120]{1,0:T(8,128)(2,1)S(1)}, u32[]{:S(2)}, u32[]{:S(2)}) collective-permute-start(bf16[64,5120]{1,0:T(8,128)(2,1)S(1)} %fusion.45), channel_id=1, source_target_pairs={{2,0},{4,2},{6,4},{3,1},{5,3},{7,5},{10,8},{12,10},{14,12},{11,9},... | collective-permute-start | bytes 1966088 | tf_op jit(solution)/shard_map/ppermute | solution.py:43
  278.7 18.7 %collective-permute-start.5 = (bf16[64,5120]{1,0:T(8,128)(2,1)S(1)}, bf16[64,5120]{1,0:T(8,128)(2,1)S(1)}, u32[]{:S(2)}, u32[]{:S(2)}) collective-permute-start(bf16[64,5120]{1,0:T(8,128)(2,1)S(1)} %fusion.51), channel_id=1, source_target_pairs={{2,0},{4,2},{6,4},{3,1},{5,3},{7,5},{10,8},{12,10},{14,12},{11,9},... | collective-permute-start | bytes 1966088 | tf_op jit(solution)/shard_map/ppermute | solution.py:43
  305.2 18.7 %collective-permute-start.6 = (bf16[64,5120]{1,0:T(8,128)(2,1)S(1)}, bf16[64,5120]{1,0:T(8,128)(2,1)S(1)}, u32[]{:S(2)}, u32[]{:S(2)}) collective-permute-start(bf16[64,5120]{1,0:T(8,128)(2,1)S(1)} %fusion.57), channel_id=1, source_target_pairs={{2,0},{4,2},{6,4},{3,1},{5,3},{7,5},{10,8},{12,10},{14,12},{11,9},... | collective-permute-start | bytes 1966088 | tf_op jit(solution)/shard_map/ppermute | solution.py:43
  331.7 18.7 %collective-permute-start.7 = (bf16[64,5120]{1,0:T(8,128)(2,1)S(1)}, bf16[64,5120]{1,0:T(8,128)(2,1)S(1)}, u32[]{:S(2)}, u32[]{:S(2)}) collective-permute-start(bf16[64,5120]{1,0:T(8,128)(2,1)S(1)} %fusion.63), channel_id=1, source_target_pairs={{2,0},{4,2},{6,4},{3,1},{5,3},{7,5},{10,8},{12,10},{14,12},{11,9},... | collective-permute-start | bytes 1966088 | tf_op jit(solution)/shard_map/ppermute | solution.py:43
  (11 other events, 18.7 us)
Sparse Core Ops, SparseCore 0:
  10.4 92.5 all-gather.1
  365.4 78.2 reduce-scatter.3
where the time goes:
time: 456 us; the launch traced here: 454 us
  waiting for transfers between devices  264 us (58%)
  blocking collectives  53.2 us (12%)
  local copies, waits for them, and re-layouts  34.1 us (7%)
  starting transfers between devices  33.1 us (7%)
  other arithmetic  33 us (7%)
  matrix products  20.9 us (5%)
  between operations  15.8 us (3%)
    ppermute x8, waiting for transfers between devices, from_behind(): return lax.ppermute(block, axis, route)  124 us
    all_gather x1, waiting for transfers between devices, turned_gather(): result = lax.all_gather(both, axis, axis=0, tiled=True)  82.5 us
    unnamed x3, waiting for transfers between devices  56.5 us
    all_to_all x8, blocking collectives, copy_for_each(): lax.all_to_all(jnp.broadcast_to(array[None], (devices, *array.shape)), ax...  53.2 us
    ppermute x8, starting transfers between devices, from_behind(): return lax.ppermute(block, axis, route)  23.9 us
    unnamed x68, local copies, waits for them, and re-layouts  13.9 us
    dynamic_update_slice x17, other arithmetic, put_slot(): lax.dynamic_update_index_in_dim(slot_store, jnp.where(active, new_value,...  11.7 us
    all_to_all x2, starting transfers between devices, copy_for_each(): lax.all_to_all(jnp.broadcast_to(array[None], (devices, *array.shape)), ax...  9.13 us
  transfers between devices with their start and end apart: 12, of which 11 were waited for; matrix products, arithmetic and copies ran while one was open for 5% of the time, Pallas kernels for 0%

commit v1 on v0

--- a/solution.py
+++ b/solution.py
@@ -12,11 +12,16 @@
 clip_low = math.log(0.8)
 
 
+def exchange_gather(value, mesh_axis, d):
+    outgoing = jnp.stack([value] * lax.axis_size(mesh_axis))
+    return jnp.concatenate(lax.all_to_all(outgoing, mesh_axis, 0, 0), axis=d)
+
+
 def turned_gather(arrays, axis, dims):
     turned = [jnp.moveaxis(a, dim, 0) for a, dim in zip(arrays, dims)]
     widths = [t[0].size for t in turned]
     both = jnp.concatenate([t.reshape(-1, w) for t, w in zip(turned, widths)], axis=1)
-    result = lax.all_gather(both, axis, axis=0, tiled=True)
+    result = exchange_gather(both, axis, 0)
     tiles = jnp.split(result, [sum(widths[:k]) for k in range(1, len(widths))], axis=1)
     return tuple(
         (

time: 456 us -> 649 us (1.42)
  waiting for transfers between devices: 264 us -> 400 us
  matrix products: 20.9 us -> 50.9 us
  starting transfers between devices: 33.1 us -> 56.5 us
    all_to_all x0 -> x1, waiting for transfers between devices: none -> 218 us  [exchange_gather(): return jnp.concatenate(lax.all_to_all(outgoing, mesh_axis, 0, 0), axis=d)]
    all_gather x1 -> x0, waiting for transfers between devices: 82.5 us -> none  [turned_gather(): result = lax.all_gather(both, axis, axis=0, tiled=True)]
    all_to_all x0 -> x1, starting transfers between devices: none -> 24.1 us  [exchange_gather(): return jnp.concatenate(lax.all_to_all(outgoing, mesh_axis, 0, 0), axis=d)]
    dot_general x9, matrix products: 6.51 us -> 22.3 us  [contract_last(): lax.dot_general(left_rows, right_rows, (((1,), (1,)), ((), ())), preferre...]
    dot_general x5, matrix products: 5.08 us -> 12.3 us  [local(): jnp.dot(normed, w_first, preferred_element_type=jnp.float32)]
    dot_general x5, matrix products: 6.27 us -> 13.2 us  [local(): jnp.dot(projected, w_second, preferred_element_type=jnp.float32)]
    unnamed x3 -> x2, waiting for transfers between devices: 56.5 us -> 57.5 us
    unnamed x68 -> x56, local copies, waits for them, and re-layouts: 13.9 us -> 13.1 us
  transfers between devices with their start and end apart: 12 -> 12, of which waited for: 11 -> 11; matrix products, arithmetic and copies ran while one was open for 5% -> 4% of each run, Pallas kernels for 0% -> 0%
where the time goes in v1:
time: 649 us; the launch traced here: 647 us
  waiting for transfers between devices  400 us (62%)
  blocking collectives  56.7 us (9%)
  starting transfers between devices  56.5 us (9%)
  matrix products  50.9 us (8%)
  local copies, waits for them, and re-layouts  36.6 us (6%)
  other arithmetic  30.4 us (5%)
  between operations  15.7 us (2%)
    all_to_all x1, waiting for transfers between devices, exchange_gather(): return jnp.concatenate(lax.all_to_all(outgoing, mesh_axis, 0, 0), axis=d)  218 us
    ppermute x8, waiting for transfers between devices, from_behind(): return lax.ppermute(block, axis, route)  124 us
    unnamed x2, waiting for transfers between devices  57.5 us
    all_to_all x8, blocking collectives, copy_for_each(): lax.all_to_all(jnp.broadcast_to(array[None], (devices, *array.shape)), ax...  56.7 us
    all_to_all x1, starting transfers between devices, exchange_gather(): return jnp.concatenate(lax.all_to_all(outgoing, mesh_axis, 0, 0), axis=d)  24.1 us
    ppermute x8, starting transfers between devices, from_behind(): return lax.ppermute(block, axis, route)  23.3 us
    dot_general x9, matrix products, contract_last(): lax.dot_general(left_rows, right_rows, (((1,), (1,)), ((), ())), preferre...  22.3 us
    dot_general x5, matrix products, local(): jnp.dot(projected, w_second, preferred_element_type=jnp.float32)  13.2 us
  transfers between devices with their start and end apart: 12, of which 11 were waited for; matrix products, arithmetic and copies ran while one was open for 4% of the time, Pallas kernels for 0%

profile of v1, /device:TPU:34, one launch (start us, length us, event | category | flops | bytes accessed | tf_op | source)
XLA Modules:
  0.0 646.7 jit_solution(6820810458116784555)
XLA Ops:
  8.3 2.9 stack.2
  11.2 24.1 %all-to-all-start = ((bf16[16,320,512]{2,1,0:T(8,128)(2,1)}), bf16[16,320,512]{2,1,0:T(8,128)(2,1)}, u32[]{:S(2)}, u32[]{:S(2)}) async-start(bf16[16,320,512]{2,1,0:T(8,128)(2,1)} %stack.2), calls=%async_computation | async-start | bytes 10485760 | tf_op jit(solution)/shard_map/all_to_all | solution.py:17
  44.6 217.8 %all-to-all-done = bf16[16,320,512]{2,1,0:T(8,128)(2,1)} async-done(((bf16[16,320,512]{2,1,0:T(8,128)(2,1)}), bf16[16,320,512]{2,1,0:T(8,128)(2,1)}, u32[]{:S(2)}, u32[]{:S(2)}) %all-to-all-start) | async-done | bytes 5242912 | tf_op jit(solution)/shard_map/all_to_all | solution.py:17
  265.0 2.7 convolution_convert_fusion.8
  267.8 4.8 all_to_all.56
  274.1 3.6 collective-permute-start
  277.8 15.0 %collective-permute-done = bf16[64,5120]{1,0:T(8,128)(2,1)S(1)} collective-permute-done((bf16[64,5120]{1,0:T(8,128)(2,1)S(1)}, bf16[64,5120]{1,0:T(8,128)(2,1)S(1)}, u32[]{:S(2)}, u32[]{:S(2)}) %collective-permute-start) | collective-permute-done | bytes 655392 | tf_op jit(solution)/shard_map/ppermute | solution.py:48
  296.3 2.6 convolution_convert_fusion.7
  300.3 4.5 all-to-all-start.2
  309.4 3.6 collective-permute-start.1
  313.1 15.0 %collective-permute-done.1 = bf16[64,5120]{1,0:T(8,128)(2,1)S(1)} collective-permute-done((bf16[64,5120]{1,0:T(8,128)(2,1)S(1)}, bf16[64,5120]{1,0:T(8,128)(2,1)S(1)}, u32[]{:S(2)}, u32[]{:S(2)}) %collective-permute-start.1) | collective-permute-done | bytes 655392 | tf_op jit(solution)/shard_map/ppermute | solution.py:48
  331.1 2.7 convolution_convert_fusion.6
  333.9 4.8 all_to_all.57
  339.2 3.6 collective-permute-start.2
  343.0 15.0 %collective-permute-done.2 = bf16[64,5120]{1,0:T(8,128)(2,1)S(1)} collective-permute-done((bf16[64,5120]{1,0:T(8,128)(2,1)S(1)}, bf16[64,5120]{1,0:T(8,128)(2,1)S(1)}, u32[]{:S(2)}, u32[]{:S(2)}) %collective-permute-start.2) | collective-permute-done | bytes 655392 | tf_op jit(solution)/shard_map/ppermute | solution.py:48
  363.7 4.8 all_to_all.58
  369.1 3.7 collective-permute-start.3
  373.8 14.0 %collective-permute-done.3 = bf16[64,5120]{1,0:T(8,128)(2,1)S(1)} collective-permute-done((bf16[64,5120]{1,0:T(8,128)(2,1)S(1)}, bf16[64,5120]{1,0:T(8,128)(2,1)S(1)}, u32[]{:S(2)}, u32[]{:S(2)}) %collective-permute-start.3) | collective-permute-done | bytes 655392 | tf_op jit(solution)/shard_map/ppermute | solution.py:48
  397.0 4.5 all-to-all-start.5
  421.2 4.8 all_to_all.59
  430.1 16.2 %collective-permute-done.4 = bf16[64,5120]{1,0:T(8,128)(2,1)S(1)} collective-permute-done((bf16[64,5120]{1,0:T(8,128)(2,1)S(1)}, bf16[64,5120]{1,0:T(8,128)(2,1)S(1)}, u32[]{:S(2)}, u32[]{:S(2)}) %collective-permute-start.4) | collective-permute-done | bytes 655392 | tf_op jit(solution)/shard_map/ppermute | solution.py:48
  449.0 2.7 convolution_convert_fusion.2
  451.8 4.8 all_to_all.60
  460.1 16.2 %collective-permute-done.5 = bf16[64,5120]{1,0:T(8,128)(2,1)S(1)} collective-permute-done((bf16[64,5120]{1,0:T(8,128)(2,1)S(1)}, bf16[64,5120]{1,0:T(8,128)(2,1)S(1)}, u32[]{:S(2)}, u32[]{:S(2)}) %collective-permute-start.5) | collective-permute-done | bytes 655392 | tf_op jit(solution)/shard_map/ppermute | solution.py:48
  481.8 4.8 all_to_all.61
  489.9 16.4 %collective-permute-done.6 = bf16[64,5120]{1,0:T(8,128)(2,1)S(1)} collective-permute-done((bf16[64,5120]{1,0:T(8,128)(2,1)S(1)}, bf16[64,5120]{1,0:T(8,128)(2,1)S(1)}, u32[]{:S(2)}, u32[]{:S(2)}) %collective-permute-start.6) | collective-permute-done | bytes 655392 | tf_op jit(solution)/shard_map/ppermute | solution.py:48
  511.8 4.8 all_to_all.62
  519.9 16.4 %collective-permute-done.7 = bf16[64,5120]{1,0:T(8,128)(2,1)S(1)} collective-permute-done((bf16[64,5120]{1,0:T(8,128)(2,1)S(1)}, bf16[64,5120]{1,0:T(8,128)(2,1)S(1)}, u32[]{:S(2)}, u32[]{:S(2)}) %collective-permute-start.7) | collective-permute-done | bytes 655392 | tf_op jit(solution)/shard_map/ppermute | solution.py:48
  542.3 2.7 pad_maximum_fusion
  545.0 7.9 %copy.34 = bf16[5120,512]{1,0:T(8,128)(2,1)} copy(bf16[5120,512]{0,1:T(8,128)(2,1)} %pad_maximum_fusion) | data formatting | bytes 10485760
  554.9 23.1 %all_to_all.63 = f32[16,1,1]{2,1,0:T(1,128)S(1)} all-to-all(f32[16,1,1]{2,1,0:T(1,128)S(1)} %broadcast_in_dim.243), channel_id=1, replica_groups=mesh['groups'=2,'dp'=16,'section'=4,'tensor'=2] {'dp'}, dimensions={0} | all-to-all | bytes 128 | tf_op jit(solution)/shard_map/all_to_all | solution.py:36
  578.6 57.5 %reduce-scatter.4.cloned.1.call-done = bf16[320,512]{1,0:T(8,128)(2,1)} async-done(((bf16[5120,512]{1,0:T(8,128)(2,1)}), bf16[320,512]{1,0:T(8,128)(2,1)}) %reduce-scatter.4.cloned.1.call-update) | async-done | bytes 327696
  (195 shorter events, 103.2 us)
Async XLA Ops:
  7.2 28.9 %copy-start = (bf16[16,8,5120]{2,1,0:T(8,128)(2,1)S(1)}, bf16[16,8,5120]{2,1,0:T(8,128)(2,1)}, u32[]{:S(2)}) copy-start(bf16[16,8,5120]{2,1,0:T(8,128)(2,1)} %param.15) | copy-start | bytes 3932164
  11.2 24.2 %copy-start.24 = (s32[16]{0:T(128)S(1)}, s32[16]{0:T(128)}, u32[]{:S(2)}) copy-start(s32[16]{0:T(128)} %param.22) | copy-start | bytes 196
  11.2 24.2 %copy-start.2 = (f32[16]{0:T(128)S(1)}, f32[16]{0:T(128)}, u32[]{:S(2)}) copy-start(f32[16]{0:T(128)} %param.23) | copy-start | bytes 196
  11.2 251.3 %all-to-all-start = ((bf16[16,320,512]{2,1,0:T(8,128)(2,1)}), bf16[16,320,512]{2,1,0:T(8,128)(2,1)}, u32[]{:S(2)}, u32[]{:S(2)}) async-start(bf16[16,320,512]{2,1,0:T(8,128)(2,1)} %stack.2), calls=%async_computation | async-start | bytes 10485760 | tf_op jit(solution)/shard_map/all_to_all | solution.py:17
  37.8 2.4 copy-start.22
  37.8 3.1 copy-start.23
  37.8 4.0 copy-start.17
  43.7 218.8 %copy-start.18 = (f32[1,5120]{1,0:T(1,128)S(1)}, f32[1,5120]{1,0:T(1,128)}, u32[]{:S(2)}) copy-start(f32[1,5120]{1,0:T(1,128)} %param.19) | copy-start | bytes 61444
  274.1 18.7 %collective-permute-start = (bf16[64,5120]{1,0:T(8,128)(2,1)S(1)}, bf16[64,5120]{1,0:T(8,128)(2,1)S(1)}, u32[]{:S(2)}, u32[]{:S(2)}) collective-permute-start(bf16[64,5120]{1,0:T(8,128)(2,1)S(1)} %fusion.21), channel_id=1, source_target_pairs={{0,2},{2,4},{4,6},{1,3},{3,5},{5,7},{8,10},{10,12},{12,14},{9,11},... | collective-permute-start | bytes 1966088 | tf_op jit(solution)/shard_map/ppermute | solution.py:48
  293.5 5.5 copy-start.4
  300.3 7.0 %all-to-all-start.2 = ((bf16[2,64,5120]{2,1,0:T(8,128)(2,1)}), bf16[2,64,5120]{2,1,0:T(8,128)(2,1)}, u32[]{:S(2)}, u32[]{:S(2)}) async-start(bf16[2,64,5120]{2,1,0:T(8,128)(2,1)} %broadcast_in_dim.206), calls=%async_computation.2 | async-start | bytes 2621440 | tf_op jit(solution)/shard_map/all_to_all | solution.py:36
  307.2 1.9 copy-start.20
  309.4 18.7 %collective-permute-start.1 = (bf16[64,5120]{1,0:T(8,128)(2,1)S(1)}, bf16[64,5120]{1,0:T(8,128)(2,1)S(1)}, u32[]{:S(2)}, u32[]{:S(2)}) collective-permute-start(bf16[64,5120]{1,0:T(8,128)(2,1)S(1)} %get-tuple-element.43), channel_id=1, source_target_pairs={{0,2},{2,4},{4,6},{1,3},{3,5},{5,7},{8,10},{10,12},{12,14},{9,11},... | collective-permute-start | bytes 1966088 | tf_op jit(solution)/shard_map/ppermute | solution.py:48
  313.0 15.1 %copy-start.10 = (bf16[16,8,5120]{2,1,0:T(8,128)(2,1)S(1)}, bf16[16,8,5120]{2,1,0:T(8,128)(2,1)}, u32[]{:S(2)}) copy-start(bf16[16,8,5120]{2,1,0:T(8,128)(2,1)} %copy-done.8) | copy-start | bytes 3932164
  328.4 10.5 %copy-start.11 = (bf16[64,5120]{1,0:T(8,128)(2,1)}, bf16[64,5120]{1,0:T(8,128)(2,1)S(1)}, u32[]{:S(2)}) copy-start(bf16[64,5120]{1,0:T(8,128)(2,1)S(1)} %get-tuple-element.35) | copy-start | bytes 1966084
  339.2 18.7 %collective-permute-start.2 = (bf16[64,5120]{1,0:T(8,128)(2,1)S(1)}, bf16[64,5120]{1,0:T(8,128)(2,1)S(1)}, u32[]{:S(2)}, u32[]{:S(2)}) collective-permute-start(bf16[64,5120]{1,0:T(8,128)(2,1)S(1)} %get-tuple-element.41), channel_id=1, source_target_pairs={{0,2},{2,4},{4,6},{1,3},{3,5},{5,7},{8,10},{10,12},{12,14},{9,11},... | collective-permute-start | bytes 1966088 | tf_op jit(solution)/shard_map/ppermute | solution.py:48
  358.3 10.5 %copy-start.13 = (bf16[64,5120]{1,0:T(8,128)(2,1)}, bf16[64,5120]{1,0:T(8,128)(2,1)S(1)}, u32[]{:S(2)}) copy-start(bf16[64,5120]{1,0:T(8,128)(2,1)S(1)} %get-tuple-element.33) | copy-start | bytes 1966084
  369.1 21.3 %copy-start.6 = (bf16[2,64,5120]{2,1,0:T(8,128)(2,1)}, bf16[2,64,5120]{2,1,0:T(8,128)(2,1)S(1)}, u32[]{:S(2)}) copy-start(bf16[2,64,5120]{2,1,0:T(8,128)(2,1)S(1)} %get-tuple-element.38) | copy-start | bytes 3932164
  369.1 18.7 %collective-permute-start.3 = (bf16[64,5120]{1,0:T(8,128)(2,1)S(1)}, bf16[64,5120]{1,0:T(8,128)(2,1)S(1)}, u32[]{:S(2)}, u32[]{:S(2)}) collective-permute-start(bf16[64,5120]{1,0:T(8,128)(2,1)S(1)} %get-tuple-element.39), channel_id=1, source_target_pairs={{0,2},{2,4},{4,6},{1,3},{3,5},{5,7},{8,10},{10,12},{12,14},{9,11},... | collective-permute-start | bytes 1966088 | tf_op jit(solution)/shard_map/ppermute | solution.py:48
  390.4 2.6 copy-start.15
  397.0 13.5 %all-to-all-start.5 = ((bf16[2,64,5120]{2,1,0:T(8,128)(2,1)}), bf16[2,64,5120]{2,1,0:T(8,128)(2,1)}, u32[]{:S(2)}, u32[]{:S(2)}) async-start(bf16[2,64,5120]{2,1,0:T(8,128)(2,1)} %broadcast_in_dim.219), calls=%async_computation.5 | async-start | bytes 2621440 | tf_op jit(solution)/shard_map/all_to_all | solution.py:36
  401.5 234.5 %reduce-scatter.4.cloned.1.call-start = ((), (), s32[]{:S(2)}) async-start(), calls=%async_computation.12 | async-start | bytes 5570560
  402.7 2.3 copy-start.12
  405.1 2.3 copy-start.14
  410.5 1.9 copy-start.16
  410.5 1.9 copy-start.7
  410.5 2.1 copy-start.19
  427.6 18.7 %collective-permute-start.4 = (bf16[64,5120]{1,0:T(8,128)(2,1)S(1)}, bf16[64,5120]{1,0:T(8,128)(2,1)S(1)}, u32[]{:S(2)}, u32[]{:S(2)}) collective-permute-start(bf16[64,5120]{1,0:T(8,128)(2,1)S(1)} %fusion.45), channel_id=1, source_target_pairs={{2,0},{4,2},{6,4},{3,1},{5,3},{7,5},{10,8},{12,10},{14,12},{11,9},... | collective-permute-start | bytes 1966088 | tf_op jit(solution)/shard_map/ppermute | solution.py:48
  457.6 18.7 %collective-permute-start.5 = (bf16[64,5120]{1,0:T(8,128)(2,1)S(1)}, bf16[64,5120]{1,0:T(8,128)(2,1)S(1)}, u32[]{:S(2)}, u32[]{:S(2)}) collective-permute-start(bf16[64,5120]{1,0:T(8,128)(2,1)S(1)} %fusion.51), channel_id=1, source_target_pairs={{2,0},{4,2},{6,4},{3,1},{5,3},{7,5},{10,8},{12,10},{14,12},{11,9},... | collective-permute-start | bytes 1966088 | tf_op jit(solution)/shard_map/ppermute | solution.py:48
  487.6 18.7 %collective-permute-start.6 = (bf16[64,5120]{1,0:T(8,128)(2,1)S(1)}, bf16[64,5120]{1,0:T(8,128)(2,1)S(1)}, u32[]{:S(2)}, u32[]{:S(2)}) collective-permute-start(bf16[64,5120]{1,0:T(8,128)(2,1)S(1)} %fusion.57), channel_id=1, source_target_pairs={{2,0},{4,2},{6,4},{3,1},{5,3},{7,5},{10,8},{12,10},{14,12},{11,9},... | collective-permute-start | bytes 1966088 | tf_op jit(solution)/shard_map/ppermute | solution.py:48
  517.6 18.7 %collective-permute-start.7 = (bf16[64,5120]{1,0:T(8,128)(2,1)S(1)}, bf16[64,5120]{1,0:T(8,128)(2,1)S(1)}, u32[]{:S(2)}, u32[]{:S(2)}) collective-permute-start(bf16[64,5120]{1,0:T(8,128)(2,1)S(1)} %fusion.63), channel_id=1, source_target_pairs={{2,0},{4,2},{6,4},{3,1},{5,3},{7,5},{10,8},{12,10},{14,12},{11,9},... | collective-permute-start | bytes 1966088 | tf_op jit(solution)/shard_map/ppermute | solution.py:48
  637.2 2.6 copy-start.1
  (5 other events, 7.7 us)
Sparse Core Ops, SparseCore 0:
  553.1 82.9 reduce-scatter.3
